TPU v7x, 32 devices: a whole 2x2x4 slice. The times are simulated.
32 devices in a mesh: blk: 8 (over y, x, core), grp: 4 (over z).
Axes of the slice: x: 2, y: 2, z: 4, core: 2. Of those that a mesh axis runs over, the one named last changes fastest.
Arguments:
- images: bfloat16 [12288, 1152], P(('blk', 'grp')), may hold values from -0.71875 to 0.71875
- texts: bfloat16 [12288, 1152], P(('blk', 'grp')), may hold values from -0.71875 to 0.71875
- text_exps: int32 [96], P(('blk', 'grp')), may hold values from -1 to 1
- counts: int32 [32], P(('blk', 'grp')), may hold values from 128 to 384, as said below
- log_temp: float32 [1], replicated, may hold values from 1.1 to 2.3
- bias: float32 [1], replicated, may hold values from -6 to -4
Outputs:
- image_grad: float32 [12288, 1152], P(('blk', 'grp'))
- text_grad: float32 [12288, 1152], P(('blk', 'grp'))
- row_loss: float32 [12288], P(('blk', 'grp'))
- scalar_grads: float32 [2], replicated
Inputs may be any that keep to these rules, and one draw needn't show every extreme that they name: `counts`: each device's count lies between 128 and 384; some device has all 384 rows valid.
All inputs are finite; a program needn't handle non-finite values.
Results may differ from a plain program's by a relative error of at most 0.0095.
Values may be sent and summed in bfloat16 or wider, within the bound.
A program may use at most 128 MiB of HBM per device.

v0:
```python
import jax
import jax.numpy as jnp
from jax import lax
from jax.sharding import PartitionSpec as P

SPAN = 128
STEPS = 2


def passed_along(value, axis, steps):
    count = lax.axis_size(axis)
    pairs = [(source, (source + steps) % count) for source in range(count)]
    return lax.ppermute(value, axis, pairs)


def dequant(raw, exps):
    scale = jnp.exp2(exps.astype(jnp.float32))
    return (
        (raw.astype(jnp.float32).reshape(-1, SPAN, raw.shape[1]) * scale[:, None, None])
        .reshape(raw.shape)
        .astype(jnp.bfloat16)
    )


def on_device(images, texts, text_exps, counts, log_temp, bias):
    rows = images.shape[0]
    width = images.shape[1]
    temp = jnp.exp(log_temp[0])
    shift_b = bias[0]
    own = lax.axis_index("grp")
    image_valid = jnp.arange(rows) < counts[0]
    positive = own * rows + jnp.arange(rows)
    row_loss = jnp.zeros((rows,), jnp.float32)
    image_grad = jnp.zeros((rows, width), jnp.float32)
    sum_temp = jnp.zeros((), jnp.float32)
    sum_bias = jnp.zeros((), jnp.float32)
    partials = []
    gathered, group_counts = (
        lax.all_gather(images, "grp", axis=0, tiled=True),
        lax.all_gather(counts, "grp", axis=0, tiled=True),
    )
    group_valid = (jnp.arange(rows)[None, :] < group_counts[:, None]).reshape(-1)
    members = group_counts.shape[0]
    mine = (texts, text_exps, counts)
    current = mine
    for step in range(STEPS):
        if step == 0:
            current = (
                lax.all_gather(mine[0], "grp", axis=0, tiled=True),
                lax.all_gather(mine[1], "grp", axis=0, tiled=True),
                lax.all_gather(mine[2], "grp", axis=0, tiled=True),
            )
        else:
            current = passed_along((current[0], current[1], current[2]), "blk", 1)
        raw, exps, block_counts = current
        block = dequant(raw, exps)
        columns = block.shape[0]
        text_valid = (jnp.arange(rows)[None, :] < block_counts[:, None]).reshape(columns)
        mask = image_valid[:, None] & text_valid[None, :]
        scores = lax.dot_general(
            images, block, (((1,), (1,)), ((), ())), preferred_element_type=jnp.float32
        )
        logits = temp * scores + shift_b
        if step == 0:
            sign = jnp.where(jnp.arange(columns)[None, :] == positive[:, None], 1.0, -1.0).astype(
                jnp.float32
            )
        else:
            sign = -jnp.ones((rows, columns), jnp.float32)
        row_loss = row_loss + jnp.sum(jnp.where(mask, jax.nn.softplus(-sign * logits), 0.0), axis=1)
        dlogit = jnp.where(mask, -sign * jax.nn.sigmoid(-sign * logits), 0.0)
        dround = dlogit.astype(jnp.bfloat16)
        image_grad = image_grad + temp * jnp.dot(dround, block, preferred_element_type=jnp.float32)
        sum_temp = sum_temp + jnp.sum(dlogit * temp * scores)
        sum_bias = sum_bias + jnp.sum(dlogit)
        own_texts = lax.dynamic_slice_in_dim(block, own * rows, rows, 0)
        own_valid = lax.dynamic_slice_in_dim(text_valid, own * rows, rows, 0)
        cross = lax.dot_general(
            gathered, own_texts, (((1,), (1,)), ((), ())), preferred_element_type=jnp.float32
        )
        cross_logits = temp * cross + shift_b
        cross_mask = group_valid[:, None] & own_valid[None, :]
        if step == 0:
            cross_sign = jnp.where(
                jnp.arange(members * rows)[:, None] == positive[None, :], 1.0, -1.0
            ).astype(jnp.float32)
        else:
            cross_sign = -jnp.ones((members * rows, rows), jnp.float32)
        cross_round = jnp.where(
            cross_mask, -cross_sign * jax.nn.sigmoid(-cross_sign * cross_logits), 0.0
        ).astype(jnp.bfloat16)
        pieces = jnp.einsum(
            "grj,grd->gjd",
            cross_round.reshape(members, rows, rows),
            gathered.reshape(members, rows, width),
            preferred_element_type=jnp.float32,
        )
        partials.append(jnp.sum((temp * pieces).astype(jnp.bfloat16).astype(jnp.float32), axis=0))
    text_grad = partials[0]
    step = 1
    text_grad = text_grad + passed_along(partials[step].astype(jnp.bfloat16), "blk", -step).astype(
        jnp.float32
    )
    totals = lax.psum((sum_temp, sum_bias), ("blk", "grp"))
    scalar_grads = jnp.stack([totals[0], totals[1]])
    return (image_grad, text_grad, row_loss, scalar_grads)


def solution(mesh):
    in_specs = (
        P(("blk", "grp"), None),
        P(("blk", "grp"), None),
        P(("blk", "grp")),
        P(("blk", "grp")),
        P(),
        P(),
    )
    out_specs = (P(("blk", "grp"), None), P(("blk", "grp"), None), P(("blk", "grp")), P())
    return jax.shard_map(
        on_device, mesh=mesh, in_specs=in_specs, out_specs=out_specs, check_vma=False
    )
```

profile of v0, /device:TPU:0, one launch (start us, length us, event | category | flops | bytes accessed | tf_op | source)
XLA Modules:
  0.0 245.9 jit_solution(4361630509620185633)
XLA Ops:
  7.2 0.0 all-gather.3.cloned.1.call-start
  7.2 0.7 all-gather.3.cloned.1.call-update
  7.9 0.0 all-gather.5.cloned.1.call-start
  7.9 0.7 all-gather.5.cloned.1.call-update
  9.3 1.2 dynamic-slice
  11.2 0.8 dynamic-update-slice
  12.0 0.8 dynamic-update-slice.1
  12.8 9.9 %all-reduce.2 = (s32[12]{0:T(128)S(1)}, s32[4]{0:T(128)S(1)}) all-reduce(s32[12]{0:T(128)S(1)} %dynamic-update-slice.1, s32[4]{0:T(128)S(1)} %dynamic-update-slice), channel_id=1, replica_groups=mesh['blk'=8,'grp'=4] {'grp'}, use_global_device_ids=true, to_apply=%add.1 | all-reduce | flops 16 | bytes 128
  22.7 0.0 collective-permute-start.2
  22.7 1.6 collective-permute-start
  24.3 0.1 iota_compare_fusion.3
  24.4 0.0 copy-start.3
  25.8 0.6 dynamic_slice.12
  26.4 0.5 iota_compare_fusion.4
  26.9 0.6 iota_add_fusion
  27.5 0.1 broadcast_bitcast_fusion.1
  27.6 0.0 collective-permute-done
  27.6 0.1 iota_compare_fusion.2
  27.7 0.6 dynamic_slice.14
  28.3 0.0 collective-permute-done.2
  28.3 0.1 broadcast_bitcast_fusion
  28.3 53.9 %all-gather.3.cloned.1.call-done = bf16[1536,1152]{1,0:T(8,128)(2,1)} async-done(((bf16[384,1152]{1,0:T(8,128)(2,1)}), bf16[1536,1152]{1,0:T(8,128)(2,1)}) %all-gather.3.cloned.1.call-update) | async-done | bytes 3538960 | tf_op jit(solution)/shard_map/all_gather | solution.py:49
  82.2 0.0 copy-done.3
  82.2 0.0 copy-done.6
  82.2 0.0 collective-permute-start.1
  82.2 2.7 %multiply_convert_fusion.3 = bf16[1536,1152]{1,0:T(8,128)(2,1)S(1)} fusion(bf16[1536,1152]{1,0:T(8,128)(2,1)} %all-gather.3.cloned.1.call-done, f32[1536]{0:T(1024)S(1)} %broadcast_bitcast_fusion.1), kind=kLoop, calls=%fused_computation.4 | loop fusion | flops 5308416 | bytes 7084032 | tf_op jit(solution)/shard_map/convert_element_type | solution.py:21
  85.0 0.0 copy-done.1
  85.0 0.0 copy-start.4
  85.0 0.0 copy-start.9
  85.0 3.5 %convolution_bitcast_fusion.1 = f32[384,1536]{0,1:T(8,128)} fusion(bf16[1536,1152]{1,0:T(8,128)(2,1)S(1)} %multiply_convert_fusion.3, bf16[384,1152]{1,0:T(8,128)(2,1)S(1)} %copy-done.1), kind=kOutput, calls=%fused_computation.12 | convolution fusion | flops 1358954496 | bytes 6782976 | tf_op jit(solution)/shard_map/dot_general | solution.py:60
  88.6 63.8 %all-gather.5.cloned.1.call-done = bf16[1536,1152]{1,0:T(8,128)(2,1)} async-done(((bf16[384,1152]{1,0:T(8,128)(2,1)}), bf16[1536,1152]{1,0:T(8,128)(2,1)}) %all-gather.5.cloned.1.call-update) | async-done | bytes 3538960 | tf_op jit(solution)/shard_map/all_gather | solution.py:39
  152.3 0.0 copy-done.4
  152.3 0.0 copy-done.9
  152.4 5.3 %fusion.17 = bf16[1536,384]{1,0:T(8,128)(2,1)S(1)} fusion(bf16[1536,1152]{1,0:T(8,128)(2,1)} %all-gather.5.cloned.1.call-done, s32[384]{0:T(512)S(1)} %copy-done.9, f32[]{:T(128)} %bitcast.59, f32[]{:T(128)} %bitcast.2, pred[384]{0:T(512)(128)(4,1)} %dynamic_slice.12, pred[1536]{0:T(1024)(128)(4,1)S(1)} %copy-done.4, ...), kind=kOutput, calls=%fused_computation.33 | convolution fusion | flops 1366622208 | bytes 5607820 | tf_op jit(solution)/shard_map/dot_general | solution.py:78
  157.6 0.0 copy-done.11
  157.6 0.0 copy-start.13
  157.7 0.0 copy-start.15
  157.7 3.5 %convert_reduce_fusion = f32[384,1152]{1,0:T(8,128)} fusion(bf16[4,384,384]{2,1,0:T(8,128)(2,1)S(1)} %bitcast.63, bf16[4,384,1152]{2,1,0:T(8,128)(2,1)S(1)} %bitcast.60, f32[]{:T(128)} %bitcast.2), kind=kOutput, calls=%fused_computation.1 | convolution fusion | flops 1365590016 | bytes 6488068 | tf_op jit(solution)/shard_map/grj,grd->gjd/dot_general | solution.py:92
  161.1 0.0 copy-done.13
  161.2 0.0 copy-done.15
  161.2 3.5 %fusion.23 = f32[384,1152]{1,0:T(8,128)} fusion(bf16[1536,1152]{1,0:T(8,128)(2,1)S(1)} %multiply_convert_fusion.3, f32[384,1536]{0,1:T(8,128)S(1)} %copy-done.15, f32[]{:T(128)} %bitcast.55, f32[]{:T(128)} %bitcast.2, s32[384]{0:T(512)S(1)} %copy-done.9, pred[384]{0:T(512)(128)(4,1)S(1)} %copy-done.13, pred[1536]{0:T(1024)(128)(4,1)S(1)} %copy-done.4), kind=kOutput, calls=%fused_computation.47 | convolution fusion | flops 1366622208 | bytes 7671176 | tf_op jit(solution)/shard_map/dot_general | solution.py:73
  164.6 0.0 collective-permute-done.1
  164.7 2.7 %multiply_convert_fusion.2 = bf16[1536,1152]{1,0:T(8,128)(2,1)S(1)} fusion(bf16[1536,1152]{1,0:T(8,128)(2,1)} %collective-permute-done.1, f32[1536]{0:T(1024)S(1)} %broadcast_bitcast_fusion), kind=kLoop, calls=%fused_computation.3 | loop fusion | flops 5308416 | bytes 7084032 | tf_op jit(solution)/shard_map/convert_element_type | solution.py:21
  167.4 0.0 copy-done.2
  167.4 0.0 copy-done.5
  167.4 0.0 copy-done.7
  167.4 0.0 copy-done.10
  167.4 0.0 copy-start.12
  167.4 9.4 %multiply_reduce_fusion = (f32[]{:T(128)}, f32[]{:T(128)}, f32[384]{0:T(512)S(1)}, f32[384]{0:T(512)S(1)}, f32[]{:T(128)}, /*index=5*/f32[]{:T(128)}, f32[384,1536]{0,1:T(8,128)}) fusion(f32[]{:T(128)} %bitcast.2, f32[]{:T(128)} %bitcast.57, pred[1536]{0:T(1024)(128)(4,1)S(1)} %copy-done.7, pred[384]{0:T(512)(128)(4,1)S(1)} %copy-done.13, ...), kind=kOutput, calls=%fused_computation.37 | convolution fusion | flops 1384316160 | bytes 9150360 | tf_op jit(solution)/shard_map/dot_general | solution.py:60
  176.9 0.0 copy-done.12
  176.9 2.6 %fusion.18 = bf16[1536,384]{1,0:T(8,128)(2,1)S(1)} fusion(bf16[1536,1152]{1,0:T(8,128)(2,1)S(1)} %copy-done.11, f32[]{:T(128)} %bitcast.58, f32[]{:T(128)} %bitcast.2, pred[384]{0:T(512)(128)(4,1)S(1)} %copy-done.12, pred[1536]{0:T(1024)(128)(4,1)S(1)} %copy-done.5, bf16[1536,1152]{1,0:T(8,128)(2,1)S(1)} %multiply_convert_fusion.2, s32[]{:T(128)S(6)} %select_n.44), kind=kOutput, calls=%fused_computation.34 | convolution fusion | flops 1363673088 | bytes 5605900 | tf_op jit(solution)/shard_map/dot_general | solution.py:78
  179.5 0.0 copy-start.8
  179.5 0.0 copy-start.14
  179.5 3.2 %fusion.21 = bf16[384,1152]{1,0:T(8,128)(2,1)} fusion(bf16[4,384,384]{2,1,0:T(8,128)(2,1)S(1)} %bitcast.62, bf16[4,384,1152]{2,1,0:T(8,128)(2,1)S(1)} %bitcast.61, f32[]{:T(128)} %bitcast.2), kind=kOutput, calls=%fused_computation.45 | convolution fusion | flops 1363820544 | bytes 5603332 | tf_op jit(solution)/shard_map/grj,grd->gjd/dot_general | solution.py:92
  182.7 1.6 collective-permute-start.3
  187.0 41.6 %all-reduce.3 = (f32[1]{0:T(128)}, f32[1]{0:T(128)}) all-reduce(f32[1]{0:T(128)} %bitcast.15, f32[1]{0:T(128)} %bitcast.14), channel_id=1, replica_groups=mesh['blk'=8,'grp'=4] {'blk','grp'}, use_global_device_ids=true, to_apply=%region_9.10 | all-reduce | flops 2 | bytes 16 | tf_op jit(solution)/shard_map/psum | solution.py:104
  228.6 0.6 add.97
  229.2 1.9 pad_maximum_fusion
  231.1 0.0 copy-done.8
  231.1 0.0 copy-done.14
  231.1 5.4 %fusion = f32[384,1152]{1,0:T(8,128)} fusion(f32[384,1152]{1,0:T(8,128)} %fusion.23, bf16[1536,1152]{1,0:T(8,128)(2,1)S(1)} %multiply_convert_fusion.2, f32[]{:T(128)} %bitcast.2, f32[384,1536]{0,1:T(8,128)} %get-tuple-element.17, f32[]{:T(128)} %bitcast.56, pred[384]{0:T(512)(128)(4,1)S(1)} %copy-done.14, pred[1536]{0:T(1024)(128)(4,1)S(1)} %copy-done.8), kind=kOutput, calls=%fused_computation.10 | convolution fusion | flops 1364557824 | bytes 9439112 | tf_op jit(solution)/shard_map/dot_general | solution.py:73
  236.5 0.0 collective-permute-done.3
  236.5 0.0 copy-done
  236.5 2.6 %convert_add_fusion = f32[384,1152]{1,0:T(8,128)} fusion(f32[384,1152]{1,0:T(8,128)S(1)} %copy-done, bf16[384,1152]{1,0:T(8,128)(2,1)} %collective-permute-done.3), kind=kLoop, calls=%fused_computation.44 | loop fusion | flops 884736 | bytes 4423680 | tf_op jit(solution)/shard_map/add | solution.py:101
  (14 shorter events, 0.1 us)
Async XLA Ops:
  7.2 75.1 %all-gather.3.cloned.1.call-start = ((), (), s32[]{:S(2)}) async-start(), calls=%async_computation | async-start | bytes 4423680 | tf_op jit(solution)/shard_map/all_gather | solution.py:49
  7.9 144.4 %all-gather.5.cloned.1.call-start = ((), (), s32[]{:S(2)}) async-start(), calls=%async_computation.1 | async-start | bytes 4423680 | tf_op jit(solution)/shard_map/all_gather | solution.py:39
  22.7 5.5 %collective-permute-start.2 = (s32[12]{0:T(128)S(1)}, s32[12]{0:T(128)S(1)}, u32[]{:S(2)}, u32[]{:S(2)}) collective-permute-start(s32[12]{0:T(128)S(1)} %get-tuple-element.13), channel_id=1, source_target_pairs={{0,4},{4,8},{8,12},{12,16},{16,20},{20,24},{24,28},{28,0},{1,5},{5... | collective-permute-start | bytes 152 | tf_op jit(solution)/shard_map/ppermute | solution.py:13
  22.7 4.8 %collective-permute-start = (s32[4]{0:T(128)S(1)}, s32[4]{0:T(128)S(1)}, u32[]{:S(2)}, u32[]{:S(2)}) collective-permute-start(s32[4]{0:T(128)S(1)} %get-tuple-element.14), channel_id=1, source_target_pairs={{0,4},{4,8},{8,12},{12,16},{16,20},{20,24},{24,28},{28,0},{1,5},{5... | collective-permute-start | bytes 56 | tf_op jit(solution)/shard_map/ppermute | solution.py:13
  24.4 57.8 %copy-start.3 = (pred[1536]{0:T(1024)(128)(4,1)}, pred[1536]{0:T(1024)(128)(4,1)S(1)}, u32[]{:S(2)}) copy-start(pred[1536]{0:T(1024)(128)(4,1)S(1)} %lt.74) | copy-start | bytes 4612
  27.7 54.6 %copy-start.6 = (pred[1536]{0:T(1024)(128)(4,1)}, pred[1536]{0:T(1024)(128)(4,1)S(1)}, u32[]{:S(2)}) copy-start(pred[1536]{0:T(1024)(128)(4,1)S(1)} %lt.78) | copy-start | bytes 4612
  82.2 2.8 %copy-start.1 = (bf16[384,1152]{1,0:T(8,128)(2,1)S(1)}, bf16[384,1152]{1,0:T(8,128)(2,1)}, u32[]{:S(2)}) copy-start(bf16[384,1152]{1,0:T(8,128)(2,1)} %param.6) | copy-start | bytes 2654212
  82.2 82.4 %collective-permute-start.1 = (bf16[1536,1152]{1,0:T(8,128)(2,1)}, bf16[1536,1152]{1,0:T(8,128)(2,1)}, u32[]{:S(2)}, u32[]{:S(2)}) collective-permute-start(bf16[1536,1152]{1,0:T(8,128)(2,1)} %all-gather.3.cloned.1.call-done), channel_id=1, source_target_pairs={{0,4},{4,8},{8,12},{12,16},{16,20},{20,24},{24,28},{28,0},{1,5},{5... | collective-permute-start | bytes 10616840 | tf_op jit(solution)/shard_map/ppermute | solution.py:13
  85.0 67.4 %copy-start.4 = (pred[1536]{0:T(1024)(128)(4,1)S(1)}, pred[1536]{0:T(1024)(128)(4,1)}, u32[]{:S(2)}) copy-start(pred[1536]{0:T(1024)(128)(4,1)} %copy-done.3) | copy-start | bytes 4612
  85.0 67.3 %copy-start.9 = (s32[384]{0:T(512)S(1)}, s32[384]{0:T(512)}, u32[]{:S(2)}) copy-start(s32[384]{0:T(512)} %iota_add_fusion) | copy-start | bytes 4612
  152.4 5.3 %copy-start.11 = (bf16[1536,1152]{1,0:T(8,128)(2,1)S(1)}, bf16[1536,1152]{1,0:T(8,128)(2,1)}, u32[]{:S(2)}) copy-start(bf16[1536,1152]{1,0:T(8,128)(2,1)} %all-gather.5.cloned.1.call-done) | copy-start | bytes 10616836
  157.6 3.5 %copy-start.13 = (pred[384]{0:T(512)(128)(4,1)S(1)}, pred[384]{0:T(512)(128)(4,1)}, u32[]{:S(2)}) copy-start(pred[384]{0:T(512)(128)(4,1)} %iota_compare_fusion.4) | copy-start | bytes 1156
  157.7 3.5 %copy-start.15 = (f32[384,1536]{0,1:T(8,128)S(1)}, f32[384,1536]{0,1:T(8,128)}, u32[]{:S(2)}) copy-start(f32[384,1536]{0,1:T(8,128)} %convolution_bitcast_fusion.1) | copy-start | bytes 7077892
  164.6 2.8 %copy-start.2 = (bf16[384,1152]{1,0:T(8,128)(2,1)S(1)}, bf16[384,1152]{1,0:T(8,128)(2,1)}, u32[]{:S(2)}) copy-start(bf16[384,1152]{1,0:T(8,128)(2,1)} %param.6) | copy-start | bytes 2654212
  164.6 2.8 %copy-start.5 = (pred[1536]{0:T(1024)(128)(4,1)S(1)}, pred[1536]{0:T(1024)(128)(4,1)}, u32[]{:S(2)}) copy-start(pred[1536]{0:T(1024)(128)(4,1)} %copy-done.3) | copy-start | bytes 4612
  164.6 2.8 %copy-start.7 = (pred[1536]{0:T(1024)(128)(4,1)S(1)}, pred[1536]{0:T(1024)(128)(4,1)}, u32[]{:S(2)}) copy-start(pred[1536]{0:T(1024)(128)(4,1)} %copy-done.6) | copy-start | bytes 4612
  164.6 2.8 %copy-start.10 = (s32[384]{0:T(512)S(1)}, s32[384]{0:T(512)}, u32[]{:S(2)}) copy-start(s32[384]{0:T(512)} %iota_add_fusion) | copy-start | bytes 4612
  167.4 9.4 %copy-start.12 = (pred[384]{0:T(512)(128)(4,1)S(1)}, pred[384]{0:T(512)(128)(4,1)}, u32[]{:S(2)}) copy-start(pred[384]{0:T(512)(128)(4,1)} %dynamic_slice.14) | copy-start | bytes 1156
  179.5 51.6 %copy-start.8 = (pred[1536]{0:T(1024)(128)(4,1)S(1)}, pred[1536]{0:T(1024)(128)(4,1)}, u32[]{:S(2)}) copy-start(pred[1536]{0:T(1024)(128)(4,1)} %copy-done.6) | copy-start | bytes 4612
  179.5 51.6 %copy-start.14 = (pred[384]{0:T(512)(128)(4,1)S(1)}, pred[384]{0:T(512)(128)(4,1)}, u32[]{:S(2)}) copy-start(pred[384]{0:T(512)(128)(4,1)} %iota_compare_fusion.4) | copy-start | bytes 1156
  182.7 53.7 %collective-permute-start.3 = (bf16[384,1152]{1,0:T(8,128)(2,1)}, bf16[384,1152]{1,0:T(8,128)(2,1)}, u32[]{:S(2)}, u32[]{:S(2)}) collective-permute-start(bf16[384,1152]{1,0:T(8,128)(2,1)} %fusion.21), channel_id=1, source_target_pairs={{0,28},{4,0},{8,4},{12,8},{16,12},{20,16},{24,20},{28,24},{1,29},{... | collective-permute-start | bytes 2654216 | tf_op jit(solution)/shard_map/ppermute | solution.py:13
  231.1 5.4 %copy-start = (f32[384,1152]{1,0:T(8,128)S(1)}, f32[384,1152]{1,0:T(8,128)}, u32[]{:S(2)}) copy-start(f32[384,1152]{1,0:T(8,128)} %convert_reduce_fusion) | copy-start | bytes 5308420
Sparse Core Ops, SparseCore 0:
  9.5 72.6 all-gather.2
  83.8 68.5 all-gather.4
where the time goes:
time: 246 us
  waiting for transfers between devices  119 us (48%)
  blocking collectives  51.5 us (21%)
  matrix products  36.4 us (15%)
  between operations  19.5 us (8%)
  other arithmetic  11.8 us (5%)
  local copies, waits for them, and re-layouts  4.29 us (2%)
  starting transfers between devices  3.33 us (1%)
    all_gather x1, waiting for transfers between devices, on_device(): lax.all_gather(images, 'grp', axis=0, tiled=True)  63.8 us
    all_gather x1, waiting for transfers between devices, on_device(): lax.all_gather(mine[0], 'grp', axis=0, tiled=True)  53.9 us
    psum x1, blocking collectives, on_device(): totals = lax.psum((sum_temp, sum_bias), ('blk', 'grp'))  41.6 us
    dot_general x2, matrix products, on_device(): lax.dot_general(images, block, (((1,), (1,)), ((), ())), preferred_elemen...  13 us
    unnamed x1, blocking collectives  9.92 us
    dot_general x2, matrix products, on_device(): jnp.dot(dround, block, preferred_element_type=jnp.float32)  8.87 us
    dot_general x2, matrix products, on_device(): lax.dot_general(gathered, own_texts, (((1,), (1,)), ((), ())), preferred_...  7.88 us
    dot_general x2, matrix products, on_device(): jnp.einsum('grj,grd->gjd', cross_round.reshape(members, rows, rows), gath...  6.73 us
  transfers between devices with their start and end apart: 6, of which 2 were waited for; matrix products, arithmetic and copies ran while one was open for 13% of the time, Pallas kernels for 0%

commit v1 on v0

v1 whole, which is shorter than its diff:
```python
import functools

import jax
import jax.numpy as jnp
from jax import lax
from jax.experimental import pallas as pl
from jax.experimental.pallas import tpu as pltpu
from jax.sharding import PartitionSpec as P

MESH = pl.DeviceIdType.MESH
SPAN = 128
F32 = jnp.float32
BF16 = jnp.bfloat16


def kernel(
    B, G, C,
    scal, img, ivalid, txt, tmask,
    ig, tg, loss, sums,
    T, AQ, R, RX, M, acc, sz, sb,
    load_sem, agS, agR, xS, xR, qS, qR, rS, rR, mS, mR, szS, szR, sbS, sbR,
):
    b = lax.axis_index("blk")
    z = lax.axis_index("grp")
    rows = img.shape[0]
    nxt = lax.rem(b + 1, B)
    prv = lax.rem(b + B - 1, B)
    up = jnp.minimum(z + 1, G - 1)
    down = jnp.maximum(z - 1, 0)
    temp = scal[0]
    bias = scal[1]

    def remote(src, dst, ss, rs, dev):
        return pltpu.make_async_remote_copy(
            src_ref=src, dst_ref=dst, send_sem=ss, recv_sem=rs, device_id=dev, device_id_type=MESH
        )

    load = pltpu.make_async_copy(txt, T.at[z], load_sem)
    load.start()
    load_m = pltpu.make_async_copy(tmask, M.at[z], mR.at[0, z])
    load_m.start()

    bar = pltpu.get_barrier_semaphore()
    partners = 0
    for d in range(1, G):
        pl.semaphore_signal(bar, inc=1, device_id=(b, lax.rem(z + d, G)), device_id_type=MESH)
        partners += 1
    for d in range(1, B):
        other = lax.rem(b + d, B)
        for e in range(G if d in (1, B - 1) else 1):
            pl.semaphore_signal(bar, inc=1, device_id=(other, lax.rem(z + e, G)), device_id_type=MESH)
            partners += 1

    ig[...] = jnp.zeros_like(ig)
    loss[...] = jnp.zeros_like(loss)
    acc[...] = jnp.zeros_like(acc)
    load.wait()
    load_m.wait()
    pl.semaphore_wait(bar, partners)

    def ag(zt, c, direction):
        return remote(T.at[zt, c], T.at[zt, c], agS.at[direction, zt, c], agR.at[zt, c],
                      (b, up if direction == 0 else down))

    def xs(zt, c):
        return remote(T.at[zt, c], T.at[G + zt, c], xS.at[zt, c], xR.at[zt, c], (nxt, z))

    def qs(zt, c):
        return remote(AQ.at[G + zt, c], R.at[zt, c], qS.at[zt, c], qR.at[zt, c], (prv, z))

    def rs(zt, c, slot, direction):
        return remote(AQ.at[zt, c], RX.at[slot, c], rS.at[zt, c], rR.at[slot, c],
                      (b, up if direction == 0 else down))

    def mask_copies():
        copies = []
        for d in range(1, G):
            copies.append(remote(tmask, M.at[z], mS.at[0, d], mR.at[0, z], (b, lax.rem(z + d, G))))
        for e in range(G):
            copies.append(remote(tmask, M.at[G + z], mS.at[1, e], mR.at[1, z], (nxt, lax.rem(z + e, G))))
        return copies

    def scalar_z(d):
        return remote(acc, sz.at[z], szS.at[d], szR.at[z], (b, lax.rem(z + d, G)))

    def scalar_b(d):
        return remote(sz.at[G], sb.at[b], sbS.at[d], sbR.at[b], (lax.rem(b + d, B), z))

    masks = mask_copies()

    def item(t, kind):
        if kind == 2:
            return (t >= 0) & (t < C), jnp.clip(t, 0, C - 1), z
        n = G - 1 - z if kind == 0 else z
        safe = jnp.maximum(n, 1)
        j = t - 1
        valid = (j >= 0) & (j < C * n)
        j = jnp.clip(j, 0, C * safe - 1)
        c = lax.div(j, safe)
        off = 1 + lax.rem(j, safe)
        zt = z + off if kind == 0 else z - off
        return valid, c, jnp.clip(zt, 0, G - 1)

    def tile(step, zt, c):
        block = T[step * G + zt, c]
        scores = lax.dot_general(
            img[...], block, (((1,), (1,)), ((), ())), preferred_element_type=F32
        )
        logits = temp * scores + bias
        row = lax.broadcasted_iota(jnp.int32, (rows, SPAN), 0)
        col = lax.broadcasted_iota(jnp.int32, (rows, SPAN), 1)
        shift = (zt - z) * rows + c * SPAN + step * (G * rows * 2)
        x = jnp.where(col + shift == row, -logits, logits)
        flip = jnp.where(col + shift == row, -1.0, 1.0)
        e = jnp.exp(-jnp.abs(x))
        mask = ivalid[...] * M[step * G + zt, c][0:1, :]
        on = mask > 0.5
        soft = jnp.maximum(x, 0.0) + jnp.log1p(e)
        sig = jnp.where(x >= 0, 1.0, e) / (1.0 + e)
        dlogit = jnp.where(on, flip * sig, 0.0)
        loss[...] += jnp.where(on, soft, 0.0)
        prod = dlogit * (temp * scores)
        acc[0:8, :] += jnp.sum(prod.reshape(rows // 8, 8, SPAN), axis=0)
        acc[8:16, :] += jnp.sum(dlogit.reshape(rows // 8, 8, SPAN), axis=0)
        dround = dlogit.astype(BF16)
        ig[...] += jnp.dot(dround, block, preferred_element_type=F32)
        part = lax.dot_general(
            dround, img[...], (((0,), (0,)), ((), ())), preferred_element_type=F32
        )
        AQ[step * G + zt, c] = (temp * part).astype(BF16)

    jobs_end = C * (G - 1) + 2
    slots = C * (G - 1) + G + 2

    def slot(t, carry):
        for direction in (0, 1):
            n = z + 1 if direction == 0 else G - z
            c = lax.div(t, n)
            edge = z < G - 1 if direction == 0 else z > 0
            due = edge & (lax.rem(t, n) == 0) & (c < C)

            @pl.when(due)
            def _():
                ag(z, jnp.minimum(c, C - 1), direction).start()

        for kind in (0, 1, 2):
            valid, c, zt = item(t, kind)

            @pl.when(valid)
            def _():
                if kind != 2:
                    onward = 1 if kind == 0 else 0
                    ag(zt, c, onward).wait_recv()

                    @pl.when(z > 0 if kind == 0 else z < G - 1)
                    def _():
                        ag(zt, c, onward).start()

                xs(zt, c).start()

        @pl.when(t == 0)
        def _():
            for copy in masks:
                copy.start()
            for d in range(1, G):
                other = lax.rem(z + d, G)
                remote(tmask, M.at[other], mS.at[0, d], mR.at[0, other], (b, other)).wait_recv()
            for e in range(G):
                other = lax.rem(z + e, G)
                remote(tmask, M.at[G + other], mS.at[1, e], mR.at[1, other], (nxt, other)).wait_recv()

        def job(k, carry):
            step = 1 - lax.div(k, 3)
            kind = lax.rem(k, 3)
            tt = t - step
            v0, c0, z0 = item(tt, 0)
            v1, c1, z1 = item(tt, 1)
            v2, c2, z2 = item(tt, 2)
            c = jnp.where(kind == 0, c0, jnp.where(kind == 1, c1, c2))
            zt = jnp.where(kind == 0, z0, jnp.where(kind == 1, z1, z2))
            valid = ((kind == 0) & v0) | ((kind == 1) & v1) | ((kind == 2) & v2)

            @pl.when(valid)
            def _():
                @pl.when(step == 1)
                def _():
                    xs(zt, c).wait_recv()

                tile(step, zt, c)

                @pl.when(step == 1)
                def _():
                    qs(zt, c).start()

            return carry

        @pl.when(t < jobs_end)
        def _():
            lax.fori_loop(0, 6, job, 0)

        @pl.when((t >= 2) & (t < C + 2))
        def _():
            c = jnp.clip(t - 2, 0, C - 1)
            qs(z, c).wait_recv()
            tg[c] = AQ[z, c].astype(F32) + R[z, c].astype(F32)

        for direction in (0, 1):
            far = z if direction == 0 else G - 1 - z
            v = t - 3 - far
            vc = jnp.clip(v, 0, C * (G - 1) - 1)
            c = lax.div(vc, G - 1)
            target = lax.rem(vc, G - 1) + 1
            zt = target if direction == 0 else G - 1 - target
            live = (v >= 0) & (v < C * (G - 1)) & (target >= far)

            @pl.when(live & (target > far))
            def _():
                qs(zt, c).wait_recv()

                @pl.when(far == 0)
                def _():
                    AQ[zt, c] = (AQ[zt, c].astype(F32) + R[zt, c].astype(F32)).astype(BF16)

                @pl.when(far > 0)
                def _():
                    rs(zt, c, zt, direction).wait_recv()
                    AQ[zt, c] = (
                        AQ[zt, c].astype(F32) + R[zt, c].astype(F32) + RX[zt, c].astype(F32)
                    ).astype(BF16)

                last = target == far + 1
                where = jnp.where(last & (direction == 1), G, zt)
                rs(zt, c, where, direction).start()

            @pl.when(live & (target == far))
            def _():
                place = z if direction == 0 else G
                rs(zt, c, place, direction).wait_recv()
                tg[c] = tg[c] + RX[place, c].astype(F32)

        @pl.when(t == jobs_end)
        def _():
            for d in range(1, G):
                scalar_z(d).start()
            sz[z] = acc[...]

        @pl.when(t == jobs_end + 1)
        def _():
            for d in range(1, G):
                other = lax.rem(z + d, G)
                remote(acc, sz.at[other], szS.at[d], szR.at[other], (b, other)).wait_recv()
            total = sz[0]
            for g in range(1, G):
                total = total + sz[g]
            sz[G] = total
            sb[b] = total
            for d in range(1, B):
                scalar_b(d).start()

        return carry

    lax.fori_loop(0, slots, slot, 0)

    for d in range(1, B):
        other = lax.rem(b + d, B)
        remote(sz.at[G], sb.at[other], sbS.at[d], sbR.at[other], (other, z)).wait_recv()
    total = sb[0]
    for g in range(1, B):
        total = total + sb[g]
    sums[...] = total
    ig[...] = ig[...] * temp

    for copy in masks:
        copy.wait_send()
    for d in range(1, G):
        scalar_z(d).wait_send()
    for d in range(1, B):
        scalar_b(d).wait_send()

    def drain(i, carry):
        zt, c = lax.div(i, C), lax.rem(i, C)
        xs(zt, c).wait_send()
        qs(zt, c).wait_send()

        @pl.when(zt != z)
        def _():
            rs(zt, c, zt, 0).wait_send()

        @pl.when((zt <= z) & (z < G - 1))
        def _():
            ag(zt, c, 0).wait_send()

        @pl.when((zt >= z) & (z > 0))
        def _():
            ag(zt, c, 1).wait_send()

        return carry

    lax.fori_loop(0, G * C, drain, 0)


def on_device(B, G, images, texts, text_exps, counts, log_temp, bias):
    rows, width = images.shape
    C = rows // SPAN
    scale = jnp.exp2(text_exps.astype(F32))
    scaled = (texts.astype(F32).reshape(C, SPAN, width) * scale[:, None, None]).astype(BF16)
    scal = jnp.concatenate([jnp.exp(log_temp), bias])
    ivalid = jnp.broadcast_to(
        (jnp.arange(rows)[:, None] < counts[0]).astype(F32), (rows, SPAN)
    )
    tmask = jnp.broadcast_to(
        (jnp.arange(rows) < counts[0]).astype(F32).reshape(C, 1, SPAN), (C, 8, SPAN)
    )
    vmem = pl.BlockSpec(memory_space=pltpu.VMEM)
    hbm = pl.BlockSpec(memory_space=pl.ANY)
    dma = pltpu.SemaphoreType.DMA
    flops = 2 * G * 3 * 2 * rows * rows * width
    ig, tg, loss, sums = pl.pallas_call(
        functools.partial(kernel, B, G, C),
        out_shape=(
            jax.ShapeDtypeStruct((rows, width), F32),
            jax.ShapeDtypeStruct((C, SPAN, width), F32),
            jax.ShapeDtypeStruct((rows, SPAN), F32),
            jax.ShapeDtypeStruct((16, SPAN), F32),
        ),
        in_specs=[pl.BlockSpec(memory_space=pltpu.SMEM), vmem, vmem, hbm, vmem],
        out_specs=(vmem, vmem, vmem, vmem),
        scratch_shapes=[
            pltpu.VMEM((2 * G, C, SPAN, width), BF16),
            pltpu.VMEM((2 * G, C, SPAN, width), BF16),
            pltpu.VMEM((G, C, SPAN, width), BF16),
            pltpu.VMEM((G + 1, C, SPAN, width), BF16),
            pltpu.VMEM((2 * G, C, 8, SPAN), F32),
            pltpu.VMEM((16, SPAN), F32),
            pltpu.VMEM((G + 1, 16, SPAN), F32),
            pltpu.VMEM((B, 16, SPAN), F32),
            dma(()),
            dma((2, G, C)), dma((G, C)),
            dma((G, C)), dma((G, C)),
            dma((G, C)), dma((G, C)),
            dma((G, C)), dma((G + 1, C)),
            dma((2, G)), dma((2, G)),
            dma((G,)), dma((G,)),
            dma((B,)), dma((B,)),
        ],
        compiler_params=pltpu.CompilerParams(
            collective_id=0, has_side_effects=True, vmem_limit_bytes=61000 * 1024
        ),
        cost_estimate=pl.CostEstimate(
            flops=flops, bytes_accessed=8 * rows * width, transcendentals=0
        ),
    )(scal, images, ivalid, scaled, tmask)
    return (
        ig,
        tg.reshape(rows, width),
        jnp.sum(loss, axis=1),
        jnp.sum(sums.reshape(2, 8 * SPAN), axis=1),
    )


def solution(mesh):
    B, G = mesh.shape["blk"], mesh.shape["grp"]
    whole = P(("blk", "grp"), None)
    split = P(("blk", "grp"))
    return jax.shard_map(
        functools.partial(on_device, B, G),
        mesh=mesh,
        in_specs=(whole, whole, split, split, P(), P()),
        out_specs=(whole, whole, split, P()),
        check_vma=False,
    )
```

time: 246 us -> 160 us (0.65)
  Pallas kernels: 0 us -> 145 us
  waiting for transfers between devices: 119 us -> 0 us
  blocking collectives: 51.5 us -> 0 us
  matrix products: 36.4 us -> 0 us
  between operations: 19.5 us -> 2.63 us
  other arithmetic: 11.8 us -> 6.74 us
  starting transfers between devices: 3.33 us -> 0 us
    pallas_call x0 -> x1, Pallas kernels: none -> 145 us  [on_device(): pl.pallas_call(functools.partial(kernel, B, G, C), out_shape=(jax.ShapeDt...]
    all_gather x2 -> x0, waiting for transfers between devices: 118 us -> none  [the longest x1 63.8 us: on_device(): lax.all_gather(images, 'grp', axis=0, tiled=True)]
    psum x1 -> x0, blocking collectives: 41.6 us -> none  [on_device(): totals = lax.psum((sum_temp, sum_bias), ('blk', 'grp'))]
    dot_general x8 -> x0, matrix products: 36.4 us -> none  [the longest x2 13 us: on_device(): lax.dot_general(images, block, (((1,), (1,)), ((), ())), preferred_elemen...]
    unnamed x1 -> x0, blocking collectives: 9.92 us -> none
    add x3 -> x0, other arithmetic: 3.73 us -> none  [the longest x1 2.57 us: on_device(): text_grad + passed_along(partials[step].astype(jnp.bfloat16), 'blk', -ste...]
    ppermute x4 -> x0, starting transfers between devices: 3.26 us -> none  [passed_along(): return lax.ppermute(value, axis, pairs)]
    reduce_sum x0 -> x3, other arithmetic: none -> 3.09 us  [the longest x1 1.65 us: on_device(): jnp.sum(loss, axis=1)]
  transfers between devices with their start and end apart: 6 -> 0, of which waited for: 2 -> 0; matrix products, arithmetic and copies ran while one was open for 13% -> 0% of each run, Pallas kernels for 0% -> 0%
where the time goes in v1:
time: 160 us
  Pallas kernels  145 us (91%)
  other arithmetic  6.74 us (4%)
  local copies, waits for them, and re-layouts  5.61 us (4%)
  between operations  2.63 us (2%)
    pallas_call x1, Pallas kernels, on_device(): pl.pallas_call(functools.partial(kernel, B, G, C), out_shape=(jax.ShapeDt...  145 us
    unnamed x4, local copies, waits for them, and re-layouts  4.14 us

profile of v1, /device:TPU:0, one launch (start us, length us, event | category | flops | bytes accessed | tf_op | source)
XLA Modules:
  0.0 159.8 jit_solution(2271497555584867862)
XLA Ops:
  2.6 0.6 pad_maximum_fusion.scal
  3.2 0.7 multiply_exponential_fusion
  3.9 0.6 broadcast_in_dim.5.tmask
  4.5 0.8 broadcast_in_dim.4.ivalid
  5.3 2.4 %fusion.txt = bf16[3,128,1152]{2,1,0:T(8,128)(2,1)} fusion(bf16[3,128,1152]{2,1,0:T(8,128)(2,1)} %bitcast.7, f32[3]{0:T(128)S(1)} %multiply_exponential_fusion), kind=kLoop, calls=%fused_computation.1 | loop fusion | flops 1327104 | bytes 1769484 | tf_op jit(solution)/shard_map/convert_element_type | solution.py:306
  7.7 144.8 %shard_map.93 = (f32[384,1152]{1,0:T(8,128)}, f32[3,128,1152]{2,1,0:T(8,128)}, f32[384,128]{1,0:T(8,128)}, f32[16,128]{1,0:T(8,128)}) custom-call(f32[2]{0:T(128)} %pad_maximum_fusion.scal, bf16[384,1152]{1,0:T(8,128)(2,1)} %img.1, f32[384,128]{1,0:T(8,128)} %broadcast_in_dim.4.ivalid, bf16[3,128,1152]{2,1,0:T(8,128)(2,1)} %fusion.txt, ...), custom_call_target="tpu_custom_call" | custom-call | flops 8153726976 | bytes 3538944 | tf_op jit(solution)/shard_map/pallas_call | solution.py:318
  152.5 0.8 reduce_sum.26
  153.3 0.1 reduce_sum.27
  153.4 0.6 reduce_sum.28
  154.0 1.6 %reduce_sum.21 = f32[384]{0:T(512)} reduce(f32[384,128]{1,0:T(8,128)} %get-tuple-element.10, f32[]{:T(128)} %constant.7.clone.1), dimensions={1}, to_apply=%region_0.0 | reduce | flops 48768 | bytes 198148 | tf_op jit(solution)/shard_map/reduce_sum | solution.py:356
  155.7 0.0 copy-start
  155.7 2.9 %copy.15 = f32[384,1152]{1,0:T(8,128)} copy(f32[384,1152]{1,0:T(8,128)} %get-tuple-element.16) | data formatting | bytes 3538944
  158.6 0.0 copy-done
  158.6 1.2 copy.16
  (2 shorter events, 0.0 us)
Async XLA Ops:
  155.7 2.9 %copy-start = (f32[3,128,1152]{2,1,0:T(8,128)S(1)}, f32[3,128,1152]{2,1,0:T(8,128)}, u32[]{:S(2)}) copy-start(f32[3,128,1152]{2,1,0:T(8,128)} %get-tuple-element.9) | copy-start | bytes 5308420

commit v2 on v1

v2 whole, which is shorter than its diff:
```python
import functools

import jax
import jax.numpy as jnp
from jax import lax
from jax.experimental import pallas as pl
from jax.experimental.pallas import tpu as pltpu
from jax.sharding import PartitionSpec as P

MESH = pl.DeviceIdType.MESH
SPAN = 128
F32 = jnp.float32
BF16 = jnp.bfloat16


def kernel(
    B, G, C, L,
    scal, img, txt, info,
    ig, igr, tg, loss, sums,
    T, A, RX, X, M, gacc, gsend, lsend, lrecv, acc, sz, sb,
    load_sem, agS, agR, rS, rR, mS, mR, iS, iR, kS, kR, szS, szR, sbS, sbR,
):
    b = lax.axis_index("blk")
    z = lax.axis_index("grp")
    rows = loss.shape[0]
    nxt = lax.rem(b + 1, B)
    prv = lax.rem(b + B - 1, B)
    up = jnp.minimum(z + 1, G - 1)
    down = jnp.maximum(z - 1, 0)
    temp = scal[0]
    bias = scal[1]

    def remote(src, dst, ss, rs, dev):
        return pltpu.make_async_remote_copy(
            src_ref=src, dst_ref=dst, send_sem=ss, recv_sem=rs, device_id=dev, device_id_type=MESH
        )

    loads = [
        pltpu.make_async_copy(txt, T.at[z], load_sem.at[0]),
        pltpu.make_async_copy(info, M.at[z], load_sem.at[1]),
        pltpu.make_async_copy(img, X.at[pl.ds(0, rows)], load_sem.at[2]),
    ]
    for load in loads:
        load.start()

    bar = pltpu.get_barrier_semaphore()
    for d in range(1, G):
        pl.semaphore_signal(bar, inc=1, device_id=(b, lax.rem(z + d, G)), device_id_type=MESH)
    for d in range(1, B):
        pl.semaphore_signal(bar, inc=1, device_id=(lax.rem(b + d, B), z), device_id_type=MESH)

    gacc[...] = jnp.zeros_like(gacc)
    loss[...] = jnp.zeros_like(loss)
    lsend[...] = jnp.zeros_like(lsend)
    acc[...] = jnp.zeros_like(acc)
    tg[...] = jnp.zeros_like(tg)
    for load in loads:
        load.wait()
    pl.semaphore_wait(bar, G + B - 2)

    def ag(zt, c, direction):
        return remote(T.at[zt, c], T.at[zt, c], agS.at[direction, zt, c], agR.at[zt, c],
                      (b, up if direction == 0 else down))

    def rs(zt, c, slot, direction):
        return remote(A.at[zt, c], RX.at[slot, c], rS.at[zt, c], rR.at[slot, c],
                      (b, up if direction == 0 else down))

    def info_z(d, place, other):
        return remote(info, M.at[place], mS.at[d], mR.at[place], (b, other))

    to_prev = [
        remote(X.at[pl.ds(0, rows)], X.at[pl.ds(rows, rows)], iS.at[0], iR.at[0], (prv, z)),
        remote(info, M.at[G], iS.at[1], iR.at[1], (prv, z)),
    ]
    to_next = [
        remote(gsend, igr, kS.at[0], kR.at[0], (nxt, z)),
        remote(lsend, lrecv, kS.at[1], kR.at[1], (nxt, z)),
    ]

    def item(t, kind):
        if kind == 2:
            start = max(C * (G - 1) - C - 1, 0)
            return (t >= start) & (t < start + C), jnp.clip(t - start, 0, C - 1), z
        n = G - 1 - z if kind == 0 else z
        safe = jnp.maximum(n, 1)
        j = t - 1
        valid = (j >= 0) & (j < C * n)
        j = jnp.clip(j, 0, C * safe - 1)
        c = lax.div(j, safe)
        off = 1 + lax.rem(j, safe)
        zt = z + off if kind == 0 else z - off
        return valid, c, jnp.clip(zt, 0, G - 1)

    def tile(zt, c):
        scale = M[zt, c + 1][0:1, 0:1]
        block = (T[zt, c].astype(F32) * scale).astype(BF16)
        text_count = M[zt, 0][0:1, :]
        col = lax.broadcasted_iota(jnp.int32, (rows, SPAN), 1) + c * SPAN
        row = lax.broadcasted_iota(jnp.int32, (rows, SPAN), 0)
        col_on = col.astype(F32) < text_count
        part = None
        for step in (0, 1):
            here = pl.ds(step * rows, rows)
            scores = lax.dot_general(
                X[here, :], block, (((1,), (1,)), ((), ())), preferred_element_type=F32
            )
            scaled = temp * scores
            logits = scaled + bias
            on = col_on & (row.astype(F32) < M[z if step == 0 else G, 0][0:1, :])
            if step == 0:
                match = col + (zt - z) * rows == row
                x = jnp.where(match, -logits, logits)
            else:
                x = logits
            e = jnp.exp(-jnp.abs(x))
            soft = jnp.maximum(x, 0.0) + jnp.log1p(e)
            dlogit = jnp.where(x >= 0, 1.0, e) / (1.0 + e)
            if step == 0:
                dlogit = jnp.where(match, -dlogit, dlogit)
            dlogit = jnp.where(on, dlogit, 0.0)
            total = loss if step == 0 else lsend
            total[...] += jnp.where(on, soft, 0.0)
            acc[0:8, :] += jnp.sum((dlogit * scaled).reshape(rows // 8, 8, SPAN), axis=0)
            acc[8:16, :] += jnp.sum(dlogit.reshape(rows // 8, 8, SPAN), axis=0)
            dround = dlogit.astype(BF16)
            gacc[here, :] += jnp.dot(dround, block, preferred_element_type=F32)
            piece = lax.dot_general(
                dround, X[here, :], (((0,), (0,)), ((), ())), preferred_element_type=F32
            )
            part = piece if part is None else part + piece
        return temp * part

    jobs_end = C * (G - 1) + 1
    slots = C * (G - 1) + G + L

    def slot(t, carry):
        for direction in (0, 1):
            n = z + 1 if direction == 0 else G - z
            c = lax.div(t, n)
            edge = z < G - 1 if direction == 0 else z > 0
            due = edge & (lax.rem(t, n) == 0) & (c < C)

            @pl.when(due)
            def _():
                ag(z, jnp.minimum(c, C - 1), direction).start()

        @pl.when(t == 0)
        def _():
            for copy in reversed(to_prev):
                copy.start()
            for d in range(1, G):
                info_z(d, z, lax.rem(z + d, G)).start()
            for d in range(1, G):
                other = lax.rem(z + d, G)
                info_z(d, other, other).wait_recv()

        for kind in (0, 1):
            valid, c, zt = item(t, kind)

            @pl.when(valid)
            def _():
                onward = 1 if kind == 0 else 0
                ag(zt, c, onward).wait_recv()

                @pl.when(z > 0 if kind == 0 else z < G - 1)
                def _():
                    ag(zt, c, onward).start()

        @pl.when(t == 1)
        def _():
            for copy in to_prev:
                copy.wait_recv()

        def job(kind, carry):
            v0, c0, z0 = item(t, 0)
            v1, c1, z1 = item(t, 1)
            v2, c2, z2 = item(t, 2)
            c = jnp.where(kind == 0, c0, jnp.where(kind == 1, c1, c2))
            zt = jnp.where(kind == 0, z0, jnp.where(kind == 1, z1, z2))
            valid = ((kind == 0) & v0) | ((kind == 1) & v1) | ((kind == 2) & v2)

            @pl.when(valid)
            def _():
                part = tile(zt, c)

                @pl.when(kind == 2)
                def _():
                    tg[c] += part

                @pl.when(kind != 2)
                def _():
                    A[zt, c] = part.astype(BF16)

            return carry

        @pl.when((t < jobs_end) & (t > 0))
        def _():
            lax.fori_loop(0, 3, job, 0)

        for direction in (0, 1):
            far = z if direction == 0 else G - 1 - z
            v = t - 1 - L - far
            vc = jnp.clip(v, 0, C * (G - 1) - 1)
            c = lax.div(vc, G - 1)
            target = lax.rem(vc, G - 1) + 1
            zt = target if direction == 0 else G - 1 - target
            live = (v >= 0) & (v < C * (G - 1)) & (target >= far)

            @pl.when(live & (target > far))
            def _():
                @pl.when(far > 0)
                def _():
                    rs(zt, c, zt, direction).wait_recv()
                    A[zt, c] = (A[zt, c].astype(F32) + RX[zt, c].astype(F32)).astype(BF16)

                last = target == far + 1
                where = jnp.where(last & (direction == 1), G, zt)
                rs(zt, c, where, direction).start()

            @pl.when(live & (target == far))
            def _():
                place = z if direction == 0 else G
                rs(zt, c, place, direction).wait_recv()
                tg[c] = tg[c] + RX[place, c].astype(F32)

        @pl.when(t == jobs_end - 1)
        def _():
            for d in range(1, G):
                remote(acc, sz.at[z], szS.at[d], szR.at[z], (b, lax.rem(z + d, G))).start()
            gsend[...] = (temp * gacc[pl.ds(rows, rows), :]).astype(BF16)
            to_next[1].start()
            to_next[0].start()
            sz[z] = acc[...]

        @pl.when(t == jobs_end)
        def _():
            ig[...] = temp * gacc[pl.ds(0, rows), :]
            for d in range(1, G):
                other = lax.rem(z + d, G)
                remote(acc, sz.at[other], szS.at[d], szR.at[other], (b, other)).wait_recv()
            total = sz[0]
            for g in range(1, G):
                total = total + sz[g]
            sz[G] = total
            sb[b] = total
            for d in range(1, B):
                remote(sz.at[G], sb.at[b], sbS.at[d], sbR.at[b], (lax.rem(b + d, B), z)).start()

        return carry

    lax.fori_loop(0, slots, slot, 0)

    for d in range(1, B):
        other = lax.rem(b + d, B)
        remote(sz.at[G], sb.at[other], sbS.at[d], sbR.at[other], (other, z)).wait_recv()
    total = sb[0]
    for g in range(1, B):
        total = total + sb[g]
    sums[...] = total
    for copy in to_next:
        copy.wait_recv()
    loss[...] += lrecv[...]

    for copy in to_prev + to_next:
        copy.wait_send()
    for d in range(1, G):
        other = lax.rem(z + d, G)
        info_z(d, z, other).wait_send()
        remote(acc, sz.at[z], szS.at[d], szR.at[z], (b, other)).wait_send()
    for d in range(1, B):
        remote(sz.at[G], sb.at[b], sbS.at[d], sbR.at[b], (lax.rem(b + d, B), z)).wait_send()

    def drain(i, carry):
        zt, c = lax.div(i, C), lax.rem(i, C)

        @pl.when(zt != z)
        def _():
            rs(zt, c, zt, 0).wait_send()

        @pl.when((zt <= z) & (z < G - 1))
        def _():
            ag(zt, c, 0).wait_send()

        @pl.when((zt >= z) & (z > 0))
        def _():
            ag(zt, c, 1).wait_send()

        return carry

    lax.fori_loop(0, G * C, drain, 0)


def on_device(B, G, images, texts, text_exps, counts, log_temp, bias):
    rows, width = images.shape
    C = rows // SPAN
    scale = jnp.exp2(text_exps.astype(F32))
    scal = jnp.concatenate([jnp.exp(log_temp), bias])
    info = jnp.broadcast_to(
        jnp.concatenate([counts.astype(F32), scale])[:, None, None], (C + 1, 8, SPAN)
    )
    vmem = pl.BlockSpec(memory_space=pltpu.VMEM)
    hbm = pl.BlockSpec(memory_space=pl.ANY)
    dma = pltpu.SemaphoreType.DMA
    flops = 2 * G * 3 * 2 * rows * rows * width
    ig, igr, tg, loss, sums = pl.pallas_call(
        functools.partial(kernel, B, G, C, 0),
        out_shape=(
            jax.ShapeDtypeStruct((rows, width), F32),
            jax.ShapeDtypeStruct((rows, width), BF16),
            jax.ShapeDtypeStruct((C, SPAN, width), F32),
            jax.ShapeDtypeStruct((rows, SPAN), F32),
            jax.ShapeDtypeStruct((16, SPAN), F32),
        ),
        in_specs=[pl.BlockSpec(memory_space=pltpu.SMEM), hbm, hbm, vmem],
        out_specs=(vmem, vmem, vmem, vmem, vmem),
        scratch_shapes=[
            pltpu.VMEM((G, C, SPAN, width), BF16),
            pltpu.VMEM((G, C, SPAN, width), BF16),
            pltpu.VMEM((G + 1, C, SPAN, width), BF16),
            pltpu.VMEM((2 * rows, width), BF16),
            pltpu.VMEM((G + 1, C + 1, 8, SPAN), F32),
            pltpu.VMEM((2 * rows, width), F32),
            pltpu.VMEM((rows, width), BF16),
            pltpu.VMEM((rows, SPAN), F32),
            pltpu.VMEM((rows, SPAN), F32),
            pltpu.VMEM((16, SPAN), F32),
            pltpu.VMEM((G + 1, 16, SPAN), F32),
            pltpu.VMEM((B, 16, SPAN), F32),
            dma((3,)),
            dma((2, G, C)), dma((G, C)),
            dma((G, C)), dma((G + 1, C)),
            dma((G,)), dma((G,)),
            dma((2,)), dma((2,)),
            dma((2,)), dma((2,)),
            dma((G,)), dma((G,)),
            dma((B,)), dma((B,)),
        ],
        compiler_params=pltpu.CompilerParams(
            collective_id=0, has_side_effects=True, vmem_limit_bytes=61000 * 1024
        ),
        cost_estimate=pl.CostEstimate(
            flops=flops, bytes_accessed=8 * rows * width, transcendentals=0
        ),
    )(scal, images, texts.reshape(C, SPAN, width), info)
    return (
        ig + igr.astype(F32),
        tg.reshape(rows, width),
        jnp.sum(loss, axis=1),
        jnp.sum(sums.reshape(2, 8 * SPAN), axis=1),
    )


def solution(mesh):
    B, G = mesh.shape["blk"], mesh.shape["grp"]
    whole = P(("blk", "grp"), None)
    split = P(("blk", "grp"))
    return jax.shard_map(
        functools.partial(on_device, B, G),
        mesh=mesh,
        in_specs=(whole, whole, split, split, P(), P()),
        out_specs=(whole, whole, split, P()),
        check_vma=False,
    )
```

time: 160 us -> 130 us (0.81)
  Pallas kernels: 145 us -> 119 us
  local copies, waits for them, and re-layouts: 5.61 us -> 1.99 us
    pallas_call x1, Pallas kernels: 145 us -> 119 us  [on_device(): pl.pallas_call(functools.partial(kernel, B, G, C, 0), out_shape=(jax.Shap...]
    add x0 -> x1, other arithmetic: none -> 3.19 us  [on_device(): ig + igr.astype(F32)]
    unnamed x4 -> x7, local copies, waits for them, and re-layouts: 4.14 us -> 1.22 us
    convert_element_type x3 -> x0, other arithmetic: 2.4 us -> none  [the longest x1 2.39 us: on_device(): (texts.astype(F32).reshape(C, SPAN, width) * scale[:, None, None]).astype...]
where the time goes in v2:
time: 130 us
  Pallas kernels  119 us (92%)
  other arithmetic  5.99 us (5%)
  between operations  2.65 us (2%)
  local copies, waits for them, and re-layouts  1.99 us (2%)
    pallas_call x1, Pallas kernels, on_device(): pl.pallas_call(functools.partial(kernel, B, G, C, 0), out_shape=(jax.Shap...  119 us
    add x1, other arithmetic, on_device(): ig + igr.astype(F32)  3.19 us

profile of v2, /device:TPU:0, one launch (start us, length us, event | category | flops | bytes accessed | tf_op | source)
XLA Modules:
  0.0 129.9 jit_solution(13647911306364723818)
XLA Ops:
  2.6 0.6 pad_maximum_fusion.scal
  3.2 0.7 multiply_exponential_fusion
  3.9 0.1 pad_maximum_fusion.1
  3.9 0.7 broadcast_in_dim.2.info
  4.6 119.3 %shard_map.93 = (f32[384,1152]{1,0:T(8,128)}, bf16[384,1152]{1,0:T(8,128)(2,1)}, f32[3,128,1152]{2,1,0:T(8,128)}, f32[384,128]{1,0:T(8,128)}, f32[16,128]{1,0:T(8,128)}) custom-call(f32[2]{0:T(128)} %pad_maximum_fusion.scal, bf16[384,1152]{1,0:T(8,128)(2,1)} %img.1, bf16[3,128,1152]{2,1,0:T(8,128)(2,1)} %bitcast.3, f32[4,8,128]{2,1,0:T(8,128)} %broadcast_in_dim.2.info), custom_call_target="tpu_custom_call" | custom-call | flops 8153726976 | bytes 3538944 | tf_op jit(solution)/shard_map/pallas_call | solution.py:306
  123.9 0.0 copy-start.2
  123.9 0.0 copy-start.1
  124.0 0.0 copy-start
  124.0 3.2 %convert_add_fusion = f32[384,1152]{1,0:T(8,128)} fusion(f32[384,1152]{1,0:T(8,128)} %get-tuple-element.9, bf16[384,1152]{1,0:T(8,128)(2,1)} %get-tuple-element.10), kind=kLoop, calls=%fused_computation | loop fusion | flops 884736 | bytes 4423680 | tf_op jit(solution)/shard_map/add | solution.py:347
  127.2 0.0 copy-done.2
  127.2 0.1 reduce_sum.26
  127.3 0.1 reduce_sum.27
  127.4 0.6 reduce_sum.28
  128.0 0.0 copy-done.1
  128.0 0.7 reduce_sum.21
  128.7 0.0 copy-done
  128.7 1.2 copy.14
Async XLA Ops:
  123.9 3.2 %copy-start.2 = (f32[16,128]{1,0:T(8,128)S(1)}, f32[16,128]{1,0:T(8,128)}, u32[]{:S(2)}) copy-start(f32[16,128]{1,0:T(8,128)} %get-tuple-element.13) | copy-start | bytes 24580
  123.9 4.0 %copy-start.1 = (f32[384,128]{1,0:T(8,128)S(1)}, f32[384,128]{1,0:T(8,128)}, u32[]{:S(2)}) copy-start(f32[384,128]{1,0:T(8,128)} %get-tuple-element.12) | copy-start | bytes 589828
  124.0 4.8 %copy-start = (f32[3,128,1152]{2,1,0:T(8,128)S(1)}, f32[3,128,1152]{2,1,0:T(8,128)}, u32[]{:S(2)}) copy-start(f32[3,128,1152]{2,1,0:T(8,128)} %get-tuple-element.11) | copy-start | bytes 5308420
